TPU v7x, 16 devices: a 4x2x1 block of a 4x4x8 slice. The times are simulated.
16 devices in a mesh: rep: 2 (over y, z), dp: 8 (over x, core).
Axes of the slice: x: 4, y: 2, z: 1, core: 2. Of those that a mesh axis runs over, the one named last changes fastest.
The devices are a block of a 4x4x8 slice.
Arguments:
- x: bfloat16 [16, 2048, 512], P(('rep', 'dp')), parts along dimension 0
- dy: bfloat16 [16, 2048, 512], P(('rep', 'dp')), parts along dimension 0
- w_gate: bfloat16 [2, 512, 1664], replicated
- w_up: bfloat16 [2, 512, 1664], replicated
- w_down: bfloat16 [2, 1664, 512], replicated
- m_w_gate: float32 [2, 512, 1664], replicated
- m_w_up: float32 [2, 512, 1664], replicated
- m_w_down: float32 [2, 1664, 512], replicated
- v_w_gate: float32 [2, 512, 1664], replicated
- v_w_up: float32 [2, 512, 1664], replicated
- v_w_down: float32 [2, 1664, 512], replicated
Outputs:
- output 1: bfloat16 [4, 512, 1664], P('rep'), parts along dimension 0
- output 2: bfloat16 [4, 512, 1664], P('rep'), parts along dimension 0
- output 3: bfloat16 [4, 1664, 512], P('rep'), parts along dimension 0
- output 4: float32 [4, 512, 1664], P('rep'), parts along dimension 0
- output 5: float32 [4, 512, 1664], P('rep'), parts along dimension 0
- output 6: float32 [4, 1664, 512], P('rep'), parts along dimension 0
- output 7: float32 [4, 512, 1664], P('rep'), parts along dimension 0
- output 8: float32 [4, 512, 1664], P('rep'), parts along dimension 0
- output 9: float32 [4, 1664, 512], P('rep'), parts along dimension 0
There are 2 independent parts. A program takes and returns all parts, laid end to end along the dimension named above; an argument that names none is the same for every part.
All inputs are finite; a program needn't handle non-finite values.
Results may differ from a plain program's by a relative error of at most 0.0202.
Values are sent between devices in bfloat16 or wider.
A program may use at most 768 MiB of HBM per device.

v0:
```python
import jax
import jax.numpy as jnp
from jax import lax
from jax.experimental import pallas as pl
from jax.experimental.pallas import tpu as pltpu
from jax.sharding import PartitionSpec as P

ANY = pl.BlockSpec(memory_space=pl.ANY)
LANES = 128
BF16, F32 = jnp.bfloat16, jnp.float32
MESH = pl.DeviceIdType.MESH


def dot(a, b, dims=((1,), (0,))):
    return lax.dot_general(a, b, (dims, ((), ())), preferred_element_type=F32)


def dot_t(a, b):
    return dot(a, b, ((1,), (1,)))


def normed(h):
    wide = h.astype(F32)
    scale = lax.rsqrt(jnp.mean(wide * wide, -1, keepdims=True) + 1e-6)
    return (wide * scale).astype(BF16)


def interleaved(wg, wu, layer, to, sem):
    out = []
    for j in range(wg.shape[2] // LANES):
        for n, w in enumerate((wg, wu)):
            out.append(pltpu.make_async_copy(w.at[layer, :, pl.ds(j * LANES, LANES)], to.at[:, pl.ds((2 * j + n) * LANES, LANES)], sem))
    return out


def pairs(blocks):
    return [(at, min(2, blocks - at)) for at in range(0, blocks, 2)]


def backward_of_product(gate, up, dp):
    s = jax.nn.sigmoid(gate)
    silu = gate * s
    return silu, (dp * up * (s + silu * (1 - s))).astype(BF16), (dp * silu).astype(BF16)


def forward_kernel(x_ref, dy_ref, wg, wu, wd, a0_ref, a0t_ref, h1_ref, a1t_ref, mid0t_ref, mid1t_ref, dg_ref, du_ref, wgu, wdv, mid0, sem):
    blocks = wg.shape[2] // LANES
    gu = [interleaved(wg, wu, l, wgu.at[l], sem.at[l]) for l in range(2)]
    down = [pltpu.make_async_copy(wd.at[l], wdv.at[l], sem.at[2 + l]) for l in range(2)]
    first = pl.program_id(0) == 0

    @pl.when(first)
    def _():
        for l in range(2):
            for c in gu[l]:
                c.start()
            down[l].start()
        pltpu.make_async_copy(wgu.at[0], wgu.at[0], sem.at[0]).wait()

    x = x_ref[...]
    a0 = normed(x)
    a0_ref[...] = a0
    a0t_ref[...] = a0.T
    for j in range(blocks):
        both = dot(a0, wgu[0, :, 2 * j * LANES : 2 * (j + 1) * LANES])
        gate, up = both[:, :LANES], both[:, LANES:]
        mid = (gate * jax.nn.sigmoid(gate) * up).astype(BF16)
        mid0[:, j * LANES : (j + 1) * LANES] = mid
        mid0t_ref[j * LANES : (j + 1) * LANES, :] = mid.T

    @pl.when(first)
    def _():
        down[0].wait()

    h1 = x + dot(mid0[...], wdv[0]).astype(BF16)
    h1_ref[...] = h1
    a1 = normed(h1)
    a1t_ref[...] = a1.T

    @pl.when(first)
    def _():
        pltpu.make_async_copy(wgu.at[1], wgu.at[1], sem.at[1]).wait()
        down[1].wait()

    dy = dy_ref[...]
    for pair, width in pairs(blocks):
        dp2 = dot_t(dy, wdv[1, pair * LANES : (pair + width) * LANES, :]).astype(BF16).astype(F32)
        for j in range(pair, pair + width):
            at = slice(j * LANES, (j + 1) * LANES)
            both = dot(a1, wgu[1, :, 2 * j * LANES : 2 * (j + 1) * LANES])
            gate, up = both[:, :LANES], both[:, LANES:]
            silu, dg, du = backward_of_product(gate, up, dp2[:, (j - pair) * LANES : (j - pair + 1) * LANES])
            mid1t_ref[at, :] = (silu * up).astype(BF16).T
            dg_ref[:, at], du_ref[:, at] = dg, du


def forward(x, dy, wg, wu, wd, bt=256):
    t, d = x.shape
    ff = wg.shape[-1]
    rows = lambda n: pl.BlockSpec((bt, n), lambda i: (i, 0))
    cols = lambda n: pl.BlockSpec((n, bt), lambda i: (0, i))
    shape = lambda *s: jax.ShapeDtypeStruct(s, BF16)
    return pl.pallas_call(
        forward_kernel,
        grid=(t // bt,),
        in_specs=[rows(d), rows(d), ANY, ANY, ANY],
        out_specs=[rows(d), cols(d), rows(d), cols(d), cols(ff), cols(ff), rows(ff), rows(ff)],
        out_shape=[shape(t, d), shape(d, t), shape(t, d), shape(d, t), shape(ff, t), shape(ff, t), shape(t, ff), shape(t, ff)],
        scratch_shapes=[
            pltpu.VMEM((2, d, 2 * ff), BF16),
            pltpu.VMEM((2, ff, d), BF16),
            pltpu.VMEM((bt, ff), BF16),
            pltpu.SemaphoreType.DMA((4,)),
        ],
        compiler_params=pltpu.CompilerParams(dimension_semantics=("arbitrary",), vmem_limit_bytes=60 * 2**20),
        name="forward",
    )(x, dy, wg, wu, wd)


ORDER = ((True, 0, 1), (False, 0, 1), (False, 1, 1), (True, 1, 0), (False, 2, 0), (False, 3, 0))
S0, X1, X2, Y2, Y1, Y0 = 0, 1, 3, 5, 7, 9


def backward_kernel(
    a0, a0t, h1, a1t, mid0t, mid1t, dg1, du1, dy, wg, wu, wd,
    out_g, out_u, out_d,
    gg, gd, r0g, r0d, r1g, r1d, r2g, r2d,
    midt, dgu, at, av, dh, hv, wgu0, wgu1, wd0,
    load, store, send, recv, credit,
):
    t, d = dh.shape
    ff = wd0.shape[0]
    blocks = ff // LANES
    bt = 256
    index = lax.axis_index("dp")
    core, chip = index % 2, index // 2
    parity = chip % 2
    chips = lax.axis_size("dp") // 2
    up_chip, down_chip = (chip + 1) % chips, (chip + chips - 1) % chips
    first_pair = jnp.where(parity == 0, up_chip, down_chip)
    second_pair = jnp.where(parity == 0, down_chip, up_chip)
    other_core = chip * 2 + 1 - core
    near = (first_pair * 2 + core, second_pair * 2 + core)
    far = (near[1], near[0])
    middle = ((chip + 1) % chips) // 2
    keep = (middle, chip // 2)
    quarter = parity

    def height(m):
        return ff if ORDER[m][0] else d // 2

    def g_ref(m, half, start, size):
        is_down, i, _ = ORDER[m]
        if is_down:
            return gd.at[i, half, pl.ds(pl.multiple_of(start, 16), size), :]
        return gg.at[i, pl.ds(pl.multiple_of(half * (d // 2) + start, 16), size), :]

    def ref_of(m, down_ref, other_ref, *at):
        is_down, i, _ = ORDER[m]
        return (down_ref if is_down else other_ref).at[(i, *at)]

    def part(ref, start, size):
        return ref.at[pl.ds(pl.multiple_of(start, 16), size), :]

    def copy(m, kind, src, dst, device):
        return pltpu.make_async_remote_copy(
            src_ref=src, dst_ref=dst, send_sem=send.at[m, kind], recv_sem=recv.at[m, kind], device_id={"dp": device}, device_id_type=MESH
        )

    def sub_at(m, ab, which):
        sub = height(m) // 4
        return ab * 2 * sub + which * sub

    def s0(m):
        return copy(m, S0, g_ref(m, 1 - core, 0, height(m)), ref_of(m, r0d, r0g), other_core)

    def x1(m, ab):
        sub = height(m) // 4
        return copy(m, X1 + ab, part(ref_of(m, r0d, r0g), sub_at(m, ab, 1 - keep[ab]), sub), ref_of(m, r1d, r1g, ab), near[ab])

    def x2(m, ab):
        q = height(m) // 8
        return copy(m, X2 + ab, part(ref_of(m, r1d, r1g, ab), (1 - quarter) * q, q), ref_of(m, r2d, r2g, ab), far[ab])

    def y2(m, ab):
        q = height(m) // 8
        ref = g_ref(m, core, sub_at(m, ab, keep[ab]) + quarter * q, q)
        return copy(m, Y2 + ab, ref, ref, far[ab])

    def y1(m, ab):
        ref = g_ref(m, core, sub_at(m, ab, keep[ab]), height(m) // 4)
        return copy(m, Y1 + ab, ref, ref, near[ab])

    def y0(m):
        ref = g_ref(m, core, 0, height(m))
        return copy(m, Y0, ref, ref, other_core)

    def outs(m):
        is_down, i, layer = ORDER[m]
        if is_down:
            return [
                pltpu.make_async_copy(gd.at[i, h], out_d.at[layer, :, pl.ds(h * (d // 2), d // 2)], store.at[m, h]) for h in range(2)
            ]
        return [pltpu.make_async_copy(gg.at[i], (out_u if i % 2 else out_g).at[layer], store.at[m, 0])]

    def added(a, b):
        return (a[...].astype(F32) + b[...].astype(F32)).astype(BF16)

    def c0(m):
        s0(m).wait_recv()
        r0 = ref_of(m, r0d, r0g)
        r0[...] = added(r0, g_ref(m, core, 0, height(m)))
        for ab in range(2):
            x1(m, ab).start()
        s0(m).wait_send()
        pl.semaphore_signal(credit.at[m], inc=1, device_id={"dp": other_core}, device_id_type=MESH)

    def c1(m):
        sub = height(m) // 4
        for ab in range(2):
            x1(m, ab).wait_recv()
            r1 = ref_of(m, r1d, r1g, ab)
            r1[...] = added(r1, part(ref_of(m, r0d, r0g), sub_at(m, ab, keep[ab]), sub))
            x2(m, ab).start()

    def c2(m):
        q = height(m) // 8
        for ab in range(2):
            x2(m, ab).wait_recv()
            to = g_ref(m, core, sub_at(m, ab, keep[ab]) + quarter * q, q)
            to[...] = added(part(ref_of(m, r1d, r1g, ab), quarter * q, q), ref_of(m, r2d, r2g, ab))
            y2(m, ab).start()

    def c3(m):
        for ab in range(2):
            y2(m, ab).wait_recv()
            y1(m, ab).start()

    def c4(m):
        for ab in range(2):
            y1(m, ab).wait_recv()
        pl.semaphore_wait(credit.at[m], 1)
        y0(m).start()

    def c5(m):
        y0(m).wait_recv()
        for c in outs(m):
            c.start()

    def finish(m):
        for ab in range(2):
            for c in (x1, x2, y2, y1):
                c(m, ab).wait_send()
        y0(m).wait_send()
        for c in outs(m):
            c.wait()

    def run(step, table):
        for when, todo in table.items():

            @pl.when(step == when)
            def _():
                for what, m in todo:
                    what(m)

    local = {
        "mid1": pltpu.make_async_copy(mid1t, midt, load.at[0]),
        "dy": pltpu.make_async_copy(dy, dh, load.at[1]),
        "a1": pltpu.make_async_copy(a1t, at, load.at[2]),
        "dg": pltpu.make_async_copy(dg1, dgu.at[0], load.at[3]),
        "du": pltpu.make_async_copy(du1, dgu.at[1], load.at[4]),
        "h1": pltpu.make_async_copy(h1, hv, load.at[5]),
        "wg1": pltpu.make_async_copy(wg.at[1], wgu1.at[0], load.at[6]),
        "wu1": pltpu.make_async_copy(wu.at[1], wgu1.at[1], load.at[7]),
        "mid0": pltpu.make_async_copy(mid0t, midt, load.at[8]),
        "wd0": pltpu.make_async_copy(wd.at[0], wd0, load.at[9]),
        "a0": pltpu.make_async_copy(a0, av, load.at[10]),
        "a0t": pltpu.make_async_copy(a0t, at, load.at[11]),
    }
    for name in ("mid1", "dy", "a1", "dg", "du", "h1", "wg1", "wu1", "wd0", "a0"):
        local[name].start()
    for c in interleaved(wg, wu, 0, wgu0, load.at[12]):
        c.start()

    barrier = pltpu.get_barrier_semaphore()
    for other in (other_core, *near):
        pl.semaphore_signal(barrier, inc=1, device_id={"dp": other}, device_id_type=MESH)

    half = d // 2

    def down_grad(m, table):
        i = ORDER[m][1]

        def body(step, carry):
            which = jnp.where(step == 0, 1 - core, core)
            gd[i, which] = dot(midt[...], dh[:, pl.ds(pl.multiple_of(which * half, half), half)]).astype(BF16)

            @pl.when(step == 0)
            def _():
                s0(m).start()

            run(step, table)
            return carry

        lax.fori_loop(0, 2, body, 0)

    def other_grads(m, table):
        i = ORDER[m][1]

        def body(step, carry):
            which = jnp.where(step % 2 == 0, 1 - core, core)
            rows = pl.ds(pl.multiple_of(which * half, half), half)
            gg[i + step // 2, rows, :] = dot(at[rows, :], dgu[step // 2]).astype(BF16)
            for n in range(2):

                @pl.when(step == 2 * n)
                def _():
                    s0(m + n).start()

            run(step, table)
            return carry

        lax.fori_loop(0, 4, body, 0)

    local["mid1"].wait()
    local["dy"].wait()
    pl.semaphore_wait(barrier, 3)
    down_grad(0, {})
    local["mid0"].start()
    local["a1"].wait()
    local["dg"].wait()
    local["du"].wait()
    other_grads(1, {0: [(c0, 0)], 2: [(c0, 1)], 3: [(c1, 0)]})
    local["a0t"].start()
    local["h1"].wait()
    local["wg1"].wait()
    local["wu1"].wait()

    def states_grad(step, carry):
        rows = pl.ds(pl.multiple_of(step * bt, bt), bt)
        by_a = dot_t(dgu[0, rows, :], wgu1[0]).astype(BF16) + dot_t(dgu[1, rows, :], wgu1[1]).astype(BF16)
        by_a = by_a.astype(F32)
        wide = hv[rows, :].astype(F32)
        scale = lax.rsqrt(jnp.mean(wide * wide, -1, keepdims=True) + 1e-6)
        along = jnp.mean(by_a * wide, -1, keepdims=True) * (scale * scale * scale)
        dh[rows, :] = dh[rows, :] + (by_a * scale - wide * along).astype(BF16)
        run(step, {0: [(c0, 2)], 3: [(c1, 1)], 4: [(c2, 0)], 6: [(c1, 2)], 7: [(c3, 0)]})
        return carry

    lax.fori_loop(0, t // bt, states_grad, 0)

    local["mid0"].wait()
    down_grad(3, {0: [(c2, 1)], 1: [(c2, 2), (c0, 3)]})
    local["wd0"].wait()
    local["a0"].wait()
    pltpu.make_async_copy(wgu0, wgu0, load.at[12]).wait()

    def layer_back(step, carry):
        rows = pl.ds(pl.multiple_of(step * bt, bt), bt)
        a, by_h = av[rows, :], dh[rows, :]
        for pair, width in pairs(blocks):
            dp2 = dot_t(by_h, wd0[pair * LANES : (pair + width) * LANES, :]).astype(BF16).astype(F32)
            for j in range(pair, pair + width):
                to = slice(j * LANES, (j + 1) * LANES)
                both = dot(a, wgu0[:, 2 * j * LANES : 2 * (j + 1) * LANES])
                _, dg, du = backward_of_product(both[:, :LANES], both[:, LANES:], dp2[:, (j - pair) * LANES : (j - pair + 1) * LANES])
                dgu[0, rows, to], dgu[1, rows, to] = dg, du
        run(step, {0: [(c4, 0)], 1: [(c3, 1)], 3: [(c1, 3)], 4: [(c3, 2)], 5: [(c5, 0)], 6: [(c4, 1)], 7: [(c2, 3)]})
        return carry

    lax.fori_loop(0, t // bt, layer_back, 0)
    local["a0t"].wait()
    other_grads(4, {0: [(c4, 2)], 1: [(c0, 4), (c5, 1)], 3: [(c0, 5), (c3, 3)]})
    tail = [(c1, 4), (c5, 2), (c1, 5), (c4, 3), (c2, 4), (c5, 3), (c2, 5), (c3, 4), (c3, 5), (c4, 4), (c5, 4), (c4, 5), (c5, 5)]
    for what, m in tail:
        what(m)
    for m in range(6):
        finish(m)


def backward(a0, a0t, h1, a1t, mid0t, mid1t, dg1, du1, dy, wg, wu, wd):
    t, d = dy.shape
    layers, _, ff = wg.shape
    half = d // 2
    vmem = lambda *s: pltpu.VMEM(s, BF16)
    return pl.pallas_call(
        backward_kernel,
        in_specs=[ANY] * 12,
        out_specs=[ANY] * 3,
        out_shape=[jax.ShapeDtypeStruct(w.shape, BF16) for w in (wg, wu, wd)],
        scratch_shapes=[
            vmem(4, d, ff),
            vmem(2, 2, ff, half),
            vmem(4, half, ff),
            vmem(2, ff, half),
            vmem(4, 2, half // 4, ff),
            vmem(2, 2, ff // 4, half),
            vmem(4, 2, half // 8, ff),
            vmem(2, 2, ff // 8, half),
            vmem(ff, t),
            vmem(2, t, ff),
            vmem(d, t),
            vmem(t, d),
            vmem(t, d),
            vmem(t, d),
            vmem(d, 2 * ff),
            vmem(2, d, ff),
            vmem(ff, d),
            pltpu.SemaphoreType.DMA((13,)),
            pltpu.SemaphoreType.DMA((6, 2)),
            pltpu.SemaphoreType.DMA((6, 10)),
            pltpu.SemaphoreType.DMA((6, 10)),
            pltpu.SemaphoreType.REGULAR((6,)),
        ],
        compiler_params=pltpu.CompilerParams(collective_id=0, has_side_effects=True, vmem_limit_bytes=67043328),
        name="backward",
    )(a0, a0t, h1, a1t, mid0t, mid1t, dg1, du1, dy, wg, wu, wd)


def adamw_kernel(*refs):
    ins, outs = refs[:12], refs[12:]
    for n in range(3):
        w, m, v, g = (ins[n + 3 * k][...].astype(F32) for k in range(4))
        m = 0.9 * m + 0.1 * g
        v = 0.95 * v + 0.05 * g * g
        step = m * lax.rsqrt(v + 1e-8) + 0.1 * w
        outs[n][...] = (w - 0.02 * step).astype(BF16)
        outs[n + 3][...] = m
        outs[n + 6][...] = v


def adamw(weights, m, v, g, parts=8):
    specs = [pl.BlockSpec((1, w.shape[1] // parts, w.shape[2]), lambda l, i: (l, i, 0)) for w in weights]
    shapes = [jax.ShapeDtypeStruct(w.shape, kind) for kind in (BF16, F32, F32) for w in weights]
    return pl.pallas_call(
        adamw_kernel,
        grid=(weights[0].shape[0], parts),
        in_specs=specs * 4,
        out_specs=specs * 3,
        out_shape=shapes,
        compiler_params=pltpu.CompilerParams(dimension_semantics=("arbitrary",) * 2, vmem_limit_bytes=60 * 2**20),
        name="adamw",
    )(*weights, *m, *v, *g)


def solution(mesh):
    def step(x, dy, *arrays):
        weights, m, v = (arrays[i : i + 3] for i in (0, 3, 6))
        made = forward(x[0], dy[0], *weights)
        return tuple(adamw(weights, m, v, backward(*made, dy[0], *weights)))

    return jax.shard_map(
        step,
        mesh=mesh,
        in_specs=(P(("rep", "dp"), None, None),) * 2 + (P(None, None, None),) * 9,
        out_specs=(P("rep", None, None),) * 9,
        check_vma=False,
    )
```

profile of v0, /device:TPU:113, one launch (start us, length us, event | category | flops | bytes accessed | tf_op | source)
XLA Modules:
  0.0 182.0 jit_solution(9661773251231149813)
XLA Ops:
  0.6 34.6 %forward.1 = (bf16[2048,512]{1,0:T(8,128)(2,1)}, bf16[512,2048]{1,0:T(8,128)(2,1)}, bf16[2048,512]{1,0:T(8,128)(2,1)}, bf16[512,2048]{1,0:T(8,128)(2,1)}, bf16[1...) custom-call(bf16[2048,512]{1,0:T(8,128)(2,1)} %bitcast.4, ...), custom_call_target="tpu_custom_call" | custom-call | tf_op jit(solution)/shard_map/forward/pallas_call | solution.py:103
  35.2 105.8 %backward.1 = (bf16[2,512,1664]{2,1,0:T(8,128)(2,1)}, bf16[2,512,1664]{2,1,0:T(8,128)(2,1)}, bf16[2,1664,512]{2,1,0:T(8,128)(2,1)}) custom-call(bf16[2048,512]{1,0:T(8,128)(2,1)} %get-tuple-element.20.a0, bf16[512,2048]{1,0:T(8,128)(2,1)} %get-tuple-element.21.a0t, bf16[2048,512]{1,0:T(8,128)(2,1)} %get-tuple-element.22.h1, ...), custom_call_target="tpu_custom_call" | custom-call | tf_op jit(solution)/shard_map/backward/pallas_call | solution.py:386
  141.1 40.8 %adamw.1 = (bf16[2,512,1664]{2,1,0:T(8,128)(2,1)}, bf16[2,512,1664]{2,1,0:T(8,128)(2,1)}, bf16[2,1664,512]{2,1,0:T(8,128)(2,1)}, f32[2,512,1664]{2,1,0:T(8,128)}...) custom-call(bf16[2,512,1664]{2,1,0:T(8,128)(2,1)} %refs_0_.1, ...), custom_call_target="tpu_custom_call" | custom-call | tf_op jit(solution)/shard_map/adamw/pallas_call | solution.py:435
where the time goes:
time: 182 us
  Pallas kernels  181 us (99%)
    pallas_call x1, Pallas kernels, backward(): pl.pallas_call(backward_kernel, in_specs=[ANY] * 12, out_specs=[ANY] * 3,...  106 us
    pallas_call x1, Pallas kernels, adamw(): pl.pallas_call(adamw_kernel, grid=(weights[0].shape[0], parts), in_specs=...  40.8 us
    pallas_call x1, Pallas kernels, forward(): pl.pallas_call(forward_kernel, grid=(t // bt,), in_specs=[rows(d), rows(d...  34.6 us

commit v1 on v0

v1 whole, which is shorter than its diff:
```python
import jax
import jax.numpy as jnp
from jax import lax
from jax.experimental import pallas as pl
from jax.experimental.pallas import tpu as pltpu
from jax.sharding import PartitionSpec as P

HBM = pl.BlockSpec(memory_space=pltpu.HBM)
VMEM = pl.BlockSpec(memory_space=pltpu.VMEM)
LANES = 128
BF16, F32 = jnp.bfloat16, jnp.float32
MESH = pl.DeviceIdType.MESH


def dot(a, b, dims=((1,), (0,))):
    return lax.dot_general(a, b, (dims, ((), ())), preferred_element_type=F32)


def dot_t(a, b):
    return dot(a, b, ((1,), (1,)))


def normed(h):
    wide = h.astype(F32)
    scale = lax.rsqrt(jnp.mean(wide * wide, -1, keepdims=True) + 1e-6)
    return (wide * scale).astype(BF16)


def interleaved(wg, wu, layer, to, sem):
    out = []
    for j in range(wg.shape[2] // LANES):
        for n, w in enumerate((wg, wu)):
            out.append(pltpu.make_async_copy(w.at[layer, :, pl.ds(j * LANES, LANES)], to.at[:, pl.ds((2 * j + n) * LANES, LANES)], sem))
    return out


def pairs(blocks):
    return [(at, min(2, blocks - at)) for at in range(0, blocks, 2)]


def backward_of_product(gate, up, dp):
    s = jax.nn.sigmoid(gate)
    silu = gate * s
    return silu, (dp * up * (s + silu * (1 - s))).astype(BF16), (dp * silu).astype(BF16)


def forward_kernel(x_ref, dy_ref, wg, wu, wd, a0_ref, a0t_ref, h1_ref, a1t_ref, mid0t_ref, mid1t_ref, dg_ref, du_ref, wgu, wdv, mid0, sem):
    blocks = wg.shape[2] // LANES
    gu = [interleaved(wg, wu, l, wgu.at[l], sem.at[l]) for l in range(2)]
    down = [pltpu.make_async_copy(wd.at[l], wdv.at[l], sem.at[2 + l]) for l in range(2)]
    first = pl.program_id(0) == 0

    @pl.when(first)
    def _():
        for l in range(2):
            for c in gu[l]:
                c.start()
            down[l].start()
        pltpu.make_async_copy(wgu.at[0], wgu.at[0], sem.at[0]).wait()

    x = x_ref[...]
    a0 = normed(x)
    a0_ref[...] = a0
    a0t_ref[...] = a0.T
    for j in range(blocks):
        both = dot(a0, wgu[0, :, 2 * j * LANES : 2 * (j + 1) * LANES])
        gate, up = both[:, :LANES], both[:, LANES:]
        mid = (gate * jax.nn.sigmoid(gate) * up).astype(BF16)
        mid0[:, j * LANES : (j + 1) * LANES] = mid
        mid0t_ref[j * LANES : (j + 1) * LANES, :] = mid.T

    @pl.when(first)
    def _():
        down[0].wait()

    h1 = x + dot(mid0[...], wdv[0]).astype(BF16)
    h1_ref[...] = h1
    a1 = normed(h1)
    a1t_ref[...] = a1.T

    @pl.when(first)
    def _():
        pltpu.make_async_copy(wgu.at[1], wgu.at[1], sem.at[1]).wait()
        down[1].wait()

    dy = dy_ref[...]
    for pair, width in pairs(blocks):
        dp2 = dot_t(dy, wdv[1, pair * LANES : (pair + width) * LANES, :]).astype(BF16).astype(F32)
        for j in range(pair, pair + width):
            at = slice(j * LANES, (j + 1) * LANES)
            both = dot(a1, wgu[1, :, 2 * j * LANES : 2 * (j + 1) * LANES])
            gate, up = both[:, :LANES], both[:, LANES:]
            silu, dg, du = backward_of_product(gate, up, dp2[:, (j - pair) * LANES : (j - pair + 1) * LANES])
            mid1t_ref[at, :] = (silu * up).astype(BF16).T
            dg_ref[:, at], du_ref[:, at] = dg, du


def forward(x, dy, wg, wu, wd, bt=256):
    t, d = x.shape
    ff = wg.shape[-1]
    rows = lambda n: pl.BlockSpec((bt, n), lambda i: (i, 0))
    cols = lambda n: pl.BlockSpec((n, bt), lambda i: (0, i))
    shape = lambda *s: jax.ShapeDtypeStruct(s, BF16)
    return pl.pallas_call(
        forward_kernel,
        grid=(t // bt,),
        in_specs=[rows(d), rows(d), HBM, HBM, HBM],
        out_specs=[rows(d), cols(d), rows(d), cols(d), cols(ff), cols(ff), rows(ff), rows(ff)],
        out_shape=[shape(t, d), shape(d, t), shape(t, d), shape(d, t), shape(ff, t), shape(ff, t), shape(t, ff), shape(t, ff)],
        scratch_shapes=[
            pltpu.VMEM((2, d, 2 * ff), BF16),
            pltpu.VMEM((2, ff, d), BF16),
            pltpu.VMEM((bt, ff), BF16),
            pltpu.SemaphoreType.DMA((4,)),
        ],
        compiler_params=pltpu.CompilerParams(dimension_semantics=("arbitrary",), vmem_limit_bytes=60 * 2**20),
        name="forward",
    )(x, dy, wg, wu, wd)


ORDER = ((True, 0, 1), (False, 0, 1), (False, 1, 1), (True, 0, 0), (False, 0, 0), (False, 1, 0))
S0, X1, X2, Y2, Y1, Y0, YR = 0, 2, 4, 6, 8, 10, 12


class Places:
    def __init__(self, tokens_d, ff):
        self.d, self.ff = tokens_d, ff
        index = lax.axis_index("dp")
        self.core, chip = index % 2, index // 2
        chips = lax.axis_size("dp") // 2
        self.quarter = chip % 2
        after, before = (chip + 1) % chips, (chip + chips - 1) % chips
        first = jnp.where(self.quarter == 0, after, before)
        second = jnp.where(self.quarter == 0, before, after)
        self.other_core = chip * 2 + 1 - self.core
        self.near = (first * 2 + self.core, second * 2 + self.core)
        self.far = (self.near[1], self.near[0])
        self.keep = (((chip + 1) % chips) // 2, chip // 2)

    def height(self, m):
        return self.ff if ORDER[m][0] else self.d // 2

    def sub_at(self, m, ab, which):
        sub = self.height(m) // 4
        return (2 * ab + which) * sub

    def share(self, m, down, other, half, start, size):
        if ORDER[m][0]:
            return down.at[half, pl.ds(pl.multiple_of(start, 16), size), :]
        return other.at[ORDER[m][1], pl.ds(pl.multiple_of(half * (self.d // 2) + start, 16), size), :]

    def greet(self):
        barrier = pltpu.get_barrier_semaphore()
        for other in (self.other_core, *self.near):
            pl.semaphore_signal(barrier, inc=1, device_id={"dp": other}, device_id_type=MESH)


def part(ref, start, size):
    return ref.at[pl.ds(pl.multiple_of(start, 16), size), :]


def added(a, b):
    return (a[...].astype(F32) + b[...].astype(F32)).astype(BF16)


def backward_kernel(
    a0, a0t, h1, a1t, mid0t, mid1t, dg1, du1, dy, wg, wu, wd,
    done_g, done_d, own_g, own_d,
    gg1, gd1, gg0, gd0, r0g, r0d, r1g, r1d, r2g, r2d,
    midt, dgu, at, av, dh, hv, wgu0, wgu1, wd0,
    load, store, quarters, send, recv, credit,
):
    t, d = dh.shape
    ff = wd0.shape[0]
    blocks = ff // LANES
    bt = 256
    half = d // 2
    p = Places(d, ff)

    def g_ref(m, half, start, size):
        return p.share(m, *((gd1, gg1) if ORDER[m][2] else (gd0, gg0)), half, start, size)

    def ref_of(m, down_ref, other_ref, *at):
        is_down, i, layer = ORDER[m]
        i = layer if is_down else 2 * layer + i
        return (down_ref if is_down else other_ref).at[(i, *at)]

    def copy(m, kind, src, dst, device):
        return pltpu.make_async_remote_copy(
            src_ref=src, dst_ref=dst, send_sem=send.at[m, kind], recv_sem=recv.at[m, kind], device_id={"dp": device}, device_id_type=MESH
        )

    def s0(m, ab):
        size = p.height(m) // 2
        return copy(m, S0 + ab, g_ref(m, 1 - p.core, ab * size, size), part(ref_of(m, r0d, r0g), ab * size, size), p.other_core)

    def x1(m, ab):
        src = part(ref_of(m, r0d, r0g), p.sub_at(m, ab, 1 - p.keep[ab]), p.height(m) // 4)
        return copy(m, X1 + ab, src, ref_of(m, r1d, r1g, ab), p.near[ab])

    def x2(m, ab):
        q = p.height(m) // 8
        return copy(m, X2 + ab, part(ref_of(m, r1d, r1g, ab), (1 - p.quarter) * q, q), ref_of(m, r2d, r2g, ab), p.far[ab])

    def y2(m, ab):
        q = p.height(m) // 8
        ref = g_ref(m, p.core, p.sub_at(m, ab, p.keep[ab]) + p.quarter * q, q)
        return copy(m, Y2 + ab, ref, ref, p.far[ab])

    def y1(m, ab):
        ref = g_ref(m, p.core, p.sub_at(m, ab, p.keep[ab]), p.height(m) // 4)
        return copy(m, Y1 + ab, ref, ref, p.near[ab])

    def y0(m):
        ref = g_ref(m, p.core, 0, p.height(m))
        return copy(m, Y0, ref, ref, p.other_core)

    def out(m):
        is_down, i, _ = ORDER[m]
        if is_down:
            return pltpu.make_async_copy(gd1, done_d, store.at[m])
        return pltpu.make_async_copy(gg1.at[i], done_g.at[i], store.at[m])

    def out_quarter(m, ab):
        to = own_d.at[ab] if ORDER[m][0] else own_g.at[ORDER[m][1], ab]
        return pltpu.make_async_copy(ref_of(m, r2d, r2g, ab), to, quarters.at[m - 3, ab])

    def c0(m, parts=(0, 1)):
        size = p.height(m) // 2
        for ab in parts:
            s0(m, ab).wait_recv()
            r0 = part(ref_of(m, r0d, r0g), ab * size, size)
            r0[...] = added(r0, g_ref(m, p.core, ab * size, size))
            x1(m, ab).start()
        for ab in parts:
            s0(m, ab).wait_send()
        if ORDER[m][2] and 1 in parts:
            pl.semaphore_signal(credit.at[m], inc=1, device_id={"dp": p.other_core}, device_id_type=MESH)

    def c0a(m):
        c0(m, (0,))

    def c0b(m):
        c0(m, (1,))

    def c1(m):
        for ab in range(2):
            x1(m, ab).wait_recv()
            r1 = ref_of(m, r1d, r1g, ab)
            r1[...] = added(r1, part(ref_of(m, r0d, r0g), p.sub_at(m, ab, p.keep[ab]), p.height(m) // 4))
            x2(m, ab).start()

    def c2(m):
        q = p.height(m) // 8
        for ab in range(2):
            x2(m, ab).wait_recv()
            if ORDER[m][2]:
                to = g_ref(m, p.core, p.sub_at(m, ab, p.keep[ab]) + p.quarter * q, q)
            else:
                to = ref_of(m, r2d, r2g, ab)
            to[...] = added(part(ref_of(m, r1d, r1g, ab), p.quarter * q, q), ref_of(m, r2d, r2g, ab))
            if ORDER[m][2]:
                y2(m, ab).start()
            else:
                out_quarter(m, ab).start()

    def c3(m):
        for ab in range(2):
            y2(m, ab).wait_recv()
            y1(m, ab).start()

    def c4(m):
        for ab in range(2):
            y1(m, ab).wait_recv()
        pl.semaphore_wait(credit.at[m], 1)
        y0(m).start()

    def c5(m):
        y0(m).wait_recv()
        out(m).start()

    def finish(m):
        for ab in range(2):
            for c in (x1, x2, y2, y1) if ORDER[m][2] else (x1, x2):
                c(m, ab).wait_send()
        if ORDER[m][2]:
            y0(m).wait_send()
            out(m).wait()
        else:
            for ab in range(2):
                out_quarter(m, ab).wait()

    def run(step, table):
        for when, todo in table.items():

            @pl.when(step == when)
            def _():
                for what, m in todo:
                    what(m)

    local = {
        "mid1": pltpu.make_async_copy(mid1t, midt, load.at[0]),
        "dy": pltpu.make_async_copy(dy, dh, load.at[1]),
        "a1": pltpu.make_async_copy(a1t, at, load.at[2]),
        "dg": pltpu.make_async_copy(dg1, dgu.at[0], load.at[3]),
        "du": pltpu.make_async_copy(du1, dgu.at[1], load.at[4]),
        "h1": pltpu.make_async_copy(h1, hv, load.at[5]),
        "wg1": pltpu.make_async_copy(wg.at[1], wgu1.at[0], load.at[6]),
        "wu1": pltpu.make_async_copy(wu.at[1], wgu1.at[1], load.at[7]),
        "mid0": pltpu.make_async_copy(mid0t, midt, load.at[8]),
        "wd0": pltpu.make_async_copy(wd.at[0], wd0, load.at[9]),
        "a0": pltpu.make_async_copy(a0, av, load.at[10]),
        "a0t": pltpu.make_async_copy(a0t, at, load.at[11]),
    }
    p.greet()
    for name in ("dy", "mid1", "a1", "dg", "du", "h1", "wg1", "wu1", "wd0", "a0"):
        local[name].start()
    for c in interleaved(wg, wu, 0, wgu0, load.at[12]):
        c.start()

    def down_grad(m, gd, table):
        def body(step, carry):
            which = jnp.where(step < 2, 1 - p.core, p.core)
            rows = pl.ds(pl.multiple_of((step % 2) * (ff // 2), 16), ff // 2)
            gd[which, rows, :] = dot(midt[rows, :], dh[:, pl.ds(pl.multiple_of(which * half, half), half)]).astype(BF16)
            for ab in range(2):

                @pl.when(step == ab)
                def _():
                    s0(m, ab).start()

            run(step, table)
            return carry

        lax.fori_loop(0, 4, body, 0)

    def other_grads(m, gg, table):
        def body(step, carry):
            which = jnp.where(step % 2 == 0, 1 - p.core, p.core)
            rows = pl.ds(pl.multiple_of(which * half, half), half)
            gg[step // 2, rows, :] = dot(at[rows, :], dgu[step // 2]).astype(BF16)
            for n in range(2):

                @pl.when(step == 2 * n)
                def _():
                    for ab in range(2):
                        s0(m + n, ab).start()

            run(step, table)
            return carry

        lax.fori_loop(0, 4, body, 0)

    local["dy"].wait()
    local["mid1"].wait()
    pl.semaphore_wait(pltpu.get_barrier_semaphore(), 3)
    down_grad(0, gd1, {2: [(c0a, 0)], 3: [(c0b, 0)]})
    local["mid0"].start()
    local["a1"].wait()
    local["dg"].wait()
    local["du"].wait()
    other_grads(1, gg1, {1: [(c1, 0), (c0, 1)], 3: [(c2, 0)]})
    local["a0t"].start()
    local["h1"].wait()
    local["wg1"].wait()
    local["wu1"].wait()

    def states_grad(step, carry):
        rows = pl.ds(pl.multiple_of(step * bt, bt), bt)
        by_a = dot_t(dgu[0, rows, :], wgu1[0]).astype(BF16) + dot_t(dgu[1, rows, :], wgu1[1]).astype(BF16)
        by_a = by_a.astype(F32)
        wide = hv[rows, :].astype(F32)
        scale = lax.rsqrt(jnp.mean(wide * wide, -1, keepdims=True) + 1e-6)
        along = jnp.mean(by_a * wide, -1, keepdims=True) * (scale * scale * scale)
        dh[rows, :] = dh[rows, :] + (by_a * scale - wide * along).astype(BF16)
        run(step, {0: [(c0, 2)], 3: [(c1, 1)], 6: [(c1, 2)]})
        return carry

    lax.fori_loop(0, t // bt, states_grad, 0)

    local["mid0"].wait()
    down_grad(3, gd0, {1: [(c3, 0)], 2: [(c2, 1), (c0a, 3)], 3: [(c0b, 3)]})
    local["wd0"].wait()
    local["a0"].wait()
    pltpu.make_async_copy(wgu0, wgu0, load.at[12]).wait()

    def layer_back(step, carry):
        rows = pl.ds(pl.multiple_of(step * bt, bt), bt)
        a, by_h = av[rows, :], dh[rows, :]
        for pair, width in pairs(blocks):
            dp2 = dot_t(by_h, wd0[pair * LANES : (pair + width) * LANES, :]).astype(BF16).astype(F32)
            for j in range(pair, pair + width):
                to = slice(j * LANES, (j + 1) * LANES)
                both = dot(a, wgu0[:, 2 * j * LANES : 2 * (j + 1) * LANES])
                _, dg, du = backward_of_product(both[:, :LANES], both[:, LANES:], dp2[:, (j - pair) * LANES : (j - pair + 1) * LANES])
                dgu[0, rows, to], dgu[1, rows, to] = dg, du
        run(step, {0: [(c2, 2)], 2: [(c4, 0)], 4: [(c5, 0), (c3, 1)], 6: [(c1, 3)], 7: [(c3, 2)]})
        return carry

    lax.fori_loop(0, t // bt, layer_back, 0)
    local["a0t"].wait()
    other_grads(4, gg0, {1: [(c4, 1), (c0, 4)], 2: [(c2, 3), (c5, 1)], 3: [(c0, 5)]})
    for what, m in [(c4, 2), (c1, 4), (c5, 2), (c1, 5), (c2, 4), (c2, 5)]:
        what(m)
    for m in range(6):
        finish(m)


def backward(a0, a0t, h1, a1t, mid0t, mid1t, dg1, du1, dy, wg, wu, wd):
    t, d = dy.shape
    ff = wg.shape[2]
    half = d // 2
    vmem = lambda *s: pltpu.VMEM(s, BF16)
    return pl.pallas_call(
        backward_kernel,
        in_specs=[HBM] * 12,
        out_specs=[HBM] * 4,
        out_shape=[
            jax.ShapeDtypeStruct(s, BF16) for s in ((2, d, ff), (2, ff, half), (2, 2, half // 8, ff), (2, ff // 8, half))
        ],
        scratch_shapes=[
            vmem(2, d, ff),
            vmem(2, ff, half),
            vmem(2, d, ff),
            vmem(2, ff, half),
            vmem(4, half, ff),
            vmem(2, ff, half),
            vmem(4, 2, half // 4, ff),
            vmem(2, 2, ff // 4, half),
            vmem(4, 2, half // 8, ff),
            vmem(2, 2, ff // 8, half),
            vmem(ff, t),
            vmem(2, t, ff),
            vmem(d, t),
            vmem(t, d),
            vmem(t, d),
            vmem(t, d),
            vmem(d, 2 * ff),
            vmem(2, d, ff),
            vmem(ff, d),
            pltpu.SemaphoreType.DMA((13,)),
            pltpu.SemaphoreType.DMA((3,)),
            pltpu.SemaphoreType.DMA((3, 2)),
            pltpu.SemaphoreType.DMA((6, 11)),
            pltpu.SemaphoreType.DMA((6, 11)),
            pltpu.SemaphoreType.REGULAR((3,)),
        ],
        compiler_params=pltpu.CompilerParams(collective_id=0, has_side_effects=True, vmem_limit_bytes=67043328),
        name="backward",
    )(a0, a0t, h1, a1t, mid0t, mid1t, dg1, du1, dy, wg, wu, wd)


def update_kernel(
    quarter_g, quarter_d, done_g, done_d, wg, wu, wd, mg, mu, md, vg, vu, vd,
    fg, fd, mg_out, mu_out, md_out, vg_out, vu_out, vd_out,
    own_g, own_d, load, quarters, send, recv,
):
    d, ff = wg.shape[1:]
    half = d // 2
    p = Places(d, ff)

    def f_ref(m, half, start, size):
        layer = ORDER[m][2]
        return p.share(m, fd.at[layer], fg.at[layer], half, start, size)

    def copy(m, kind, src, dst, device):
        at = (m - 3, kind - Y2)
        return pltpu.make_async_remote_copy(
            src_ref=src, dst_ref=dst, send_sem=send.at[at], recv_sem=recv.at[at], device_id={"dp": device}, device_id_type=MESH
        )

    def own_quarter(m, ab):
        q = p.height(m) // 8
        return p.core, p.sub_at(m, ab, p.keep[ab]) + p.quarter * q, q

    def summed(m, ab):
        return quarter_d.at[ab] if ORDER[m][0] else quarter_g.at[ORDER[m][1], ab]

    def y2(m, ab):
        ref = f_ref(m, *own_quarter(m, ab))
        return copy(m, Y2 + ab, ref, ref, p.far[ab])

    def mine(m, ab):
        return pltpu.make_async_copy(summed(m, ab), f_ref(m, *own_quarter(m, ab)), quarters.at[m - 3, ab])

    def y1(m, ab):
        ref = f_ref(m, p.core, p.sub_at(m, ab, p.keep[ab]), p.height(m) // 4)
        return copy(m, Y1 + ab, ref, ref, p.near[ab])

    def y0(m, ab):
        ref = f_ref(m, p.core, p.sub_at(m, ab, p.keep[ab]), p.height(m) // 4)
        return copy(m, Y0 + ab, ref, ref, p.other_core)

    def yr(m, ab):
        ref = f_ref(m, p.core, p.sub_at(m, ab, 1 - p.keep[ab]), p.height(m) // 4)
        return copy(m, YR + ab, ref, ref, p.other_core)

    def loads(m):
        is_down, i, layer = ORDER[m]
        w, mom, var = ((wd, md, vd), (wg, mg, vg), (wu, mu, vu))[0 if is_down else 1 + i]
        mom_out, var_out = ((md_out, vd_out), (mg_out, vg_out), (mu_out, vu_out))[0 if is_down else 1 + i]
        rest = [
            pltpu.make_async_copy(mom.at[layer], mom_out.at[layer], load.at[m, 1]),
            pltpu.make_async_copy(var.at[layer], var_out.at[layer], load.at[m, 2]),
        ]
        if layer:
            if is_down:
                rest.append(pltpu.make_async_copy(done_d, fd.at[layer], load.at[m, 3]))
            else:
                rest.append(pltpu.make_async_copy(done_g.at[i], fg.at[layer, i], load.at[m, 3]))
        to = own_d if is_down else own_g.at[i]
        return pltpu.make_async_copy(w.at[layer], to, load.at[m, 0]), rest

    def adamw(m, half_of, ab, which):
        is_down, i, layer = ORDER[m]
        mom, var = ((md_out, vd_out), (mg_out, vg_out), (mu_out, vu_out))[0 if is_down else 1 + i]
        size = p.height(m) // 4
        start = p.sub_at(m, ab, which)
        if is_down:
            at = (pl.ds(pl.multiple_of(start, 16), size), pl.ds(pl.multiple_of(half_of * half, half), half))
            w = own_d[at]
        else:
            at = (pl.ds(pl.multiple_of(half_of * half + start, 16), size), slice(None))
            w = own_g[(i, *at)]
        w = w.astype(F32)
        f = f_ref(m, half_of, start, size)
        g = f[...].astype(F32)
        new_m = 0.9 * mom[(layer, *at)] + 0.1 * g
        new_v = 0.95 * var[(layer, *at)] + 0.05 * g * g
        f[...] = (w - 0.02 * (new_m * lax.rsqrt(new_v + 1e-8) + 0.1 * w)).astype(BF16)
        mom[(layer, *at)] = new_m
        var[(layer, *at)] = new_v

    def c3(m):
        q = p.height(m) // 8
        for ab in range(2):
            y2(m, ab).wait_recv()
            y1(m, ab).start()
        for ab in range(2):
            y0(m, ab).start()

    def c4(m):
        for ab in range(2):
            y1(m, ab).wait_recv()
            yr(m, ab).start()

    def whole(m):
        own, rest = loads(m)
        own.wait()
        for c in rest:
            c.wait()

        def body(n, carry):
            adamw(m, n // 4, (n // 2) % 2, n % 2)
            return carry

        lax.fori_loop(0, 8, body, 0)
        loads(m + 3)[0].start()

    def others_kept(m):
        own, rest = loads(m)
        own.wait()
        for c in rest:
            c.wait()
        for ab in range(2):
            y0(m, ab).wait_recv()
            adamw(m, 1 - p.core, ab, p.keep[ab])

    def the_rest(m):
        for ab in range(2):
            y2(m, ab).wait_send()
            y0(m, ab).wait_send()
            y1(m, ab).wait_send()
            adamw(m, p.core, ab, p.keep[ab])
        for ab in range(2):
            yr(m, ab).wait_send()
            adamw(m, p.core, ab, 1 - p.keep[ab])
        for ab in range(2):
            yr(m, ab).wait_recv()
            adamw(m, 1 - p.core, ab, 1 - p.keep[ab])

    p.greet()
    for m in (3, 4, 5):
        for ab in range(2):
            mine(m, ab).start()
    for m in range(6):
        own, rest = loads(m)
        if m < 3:
            own.start()
        for c in rest:
            c.start()
    pl.semaphore_wait(pltpu.get_barrier_semaphore(), 3)
    for m in (3, 4, 5):
        for ab in range(2):
            mine(m, ab).wait()
            y2(m, ab).start()
    whole(0)
    c3(3)
    whole(1)
    c3(4)
    whole(2)
    c3(5)
    others_kept(3)
    c4(3)
    the_rest(3)
    others_kept(4)
    c4(4)
    the_rest(4)
    others_kept(5)
    c4(5)
    the_rest(5)


def update(weights, m, v, done_g, done_d, own_g, own_d):
    _, d, ff = weights[0].shape
    half = d // 2
    return pl.pallas_call(
        update_kernel,
        in_specs=[HBM] * 13,
        out_specs=[VMEM] * 8,
        out_shape=[pltpu.VMEM((2, 2, d, ff), BF16), pltpu.VMEM((2, 2, ff, half), BF16)] + [pltpu.VMEM(one.shape, F32) for one in (*m, *v)],
        scratch_shapes=[
            pltpu.VMEM((2, d, ff), BF16),
            pltpu.VMEM((ff, d), BF16),
            pltpu.SemaphoreType.DMA((6, 4)),
            pltpu.SemaphoreType.DMA((3, 2)),
            pltpu.SemaphoreType.DMA((3, 8)),
            pltpu.SemaphoreType.DMA((3, 8)),
        ],
        compiler_params=pltpu.CompilerParams(collective_id=1, has_side_effects=True, vmem_limit_bytes=12 * 2**20),
        name="update",
    )(own_g, own_d, done_g, done_d, *weights, *m, *v)


def written_kernel(fg, fd, mg, mu, md, vg, vu, vd, wg_out, wu_out, wd_out, mg_out, mu_out, md_out, vg_out, vu_out, vd_out, sem):
    layers, _, d, ff = fg.shape
    half = d // 2
    copies = [(one, to) for one, to in zip((mg, mu, md, vg, vu, vd), (mg_out, mu_out, md_out, vg_out, vu_out, vd_out), strict=True)]
    for l in range(layers):
        copies += [(fg.at[l, 0], wg_out.at[l]), (fg.at[l, 1], wu_out.at[l])]
        copies += [(fd.at[l, h], wd_out.at[l, :, pl.ds(h * half, half)]) for h in range(2)]
    copies = [pltpu.make_async_copy(a, b, sem.at[n]) for n, (a, b) in enumerate(copies)]
    for c in copies:
        c.start()
    for c in copies:
        c.wait()


def written(weights, values):
    return pl.pallas_call(
        written_kernel,
        in_specs=[VMEM] * 8,
        out_specs=[HBM] * 9,
        out_shape=[jax.ShapeDtypeStruct(w.shape, kind) for kind in (BF16, F32, F32) for w in weights],
        scratch_shapes=[pltpu.SemaphoreType.DMA((14,))],
        compiler_params=pltpu.CompilerParams(vmem_limit_bytes=12 * 2**20),
        name="written",
    )(*(pltpu.with_memory_space_constraint(one, pltpu.VMEM) for one in values))


def solution(mesh):
    def step(x, dy, *arrays):
        weights, m, v = (arrays[i : i + 3] for i in (0, 3, 6))
        made = forward(x[0], dy[0], *weights)
        summed = backward(*made, dy[0], *weights)
        return tuple(written(weights, update(weights, m, v, *summed)))

    return jax.shard_map(
        step,
        mesh=mesh,
        in_specs=(P(("rep", "dp"), None, None),) * 2 + (P(None, None, None),) * 9,
        out_specs=(P("rep", None, None),) * 9,
        check_vma=False,
    )
```

time: 182 us -> 158 us (0.87)
  Pallas kernels: 181 us -> 157 us
    pallas_call x2 -> x3, Pallas kernels: 147 us -> 123 us  [the longest x1 77 us: backward(): pl.pallas_call(backward_kernel, in_specs=[HBM] * 12, out_specs=[HBM] * 4,...]
where the time goes in v1:
time: 158 us
  Pallas kernels  157 us (99%)
    pallas_call x1, Pallas kernels, backward(): pl.pallas_call(backward_kernel, in_specs=[HBM] * 12, out_specs=[HBM] * 4,...  77 us
    pallas_call x1, Pallas kernels, forward(): pl.pallas_call(forward_kernel, grid=(t // bt,), in_specs=[rows(d), rows(d...  34.6 us
    pallas_call x1, Pallas kernels, update(): pl.pallas_call(update_kernel, in_specs=[HBM] * 13, out_specs=[VMEM] * 8,...  29.3 us
    pallas_call x1, Pallas kernels, written(): pl.pallas_call(written_kernel, in_specs=[VMEM] * 8, out_specs=[HBM] * 9,...  16.3 us

profile of v1, /device:TPU:113, one launch (start us, length us, event | category | flops | bytes accessed | tf_op | source)
XLA Modules:
  0.0 158.0 jit_solution(4917388880866006091)
XLA Ops:
  0.6 34.6 %forward.1 = (bf16[2048,512]{1,0:T(8,128)(2,1)}, bf16[512,2048]{1,0:T(8,128)(2,1)}, bf16[2048,512]{1,0:T(8,128)(2,1)}, bf16[512,2048]{1,0:T(8,128)(2,1)}, bf16[1...) custom-call(bf16[2048,512]{1,0:T(8,128)(2,1)} %bitcast.4, ...), custom_call_target="tpu_custom_call" | custom-call | tf_op jit(solution)/shard_map/forward/pallas_call | solution.py:104
  35.2 77.0 %backward.1 = (bf16[2,512,1664]{2,1,0:T(8,128)(2,1)}, bf16[2,1664,256]{2,1,0:T(8,128)(2,1)}, bf16[2,2,32,1664]{3,2,1,0:T(8,128)(2,1)}, bf16[2,208,256]{2,1,0:T(8,128)(2,1)}) custom-call(bf16[2048,512]{1,0:T(8,128)(2,1)} %get-tuple-element.29.a0, bf16[512,2048]{1,0:T(8,128)(2,1)} %get-tuple-element.30.a0t, bf16[2048,512]{1,0:T(8,128)(2,1)} %get-tuple-element.31.h1, ...), custom_call_target="tpu_custom_call" | custom-call | tf_op jit(solution)/shard_map/backward/pallas_call | solution.py:414
  112.2 29.3 %update.1 = (bf16[2,2,512,1664]{3,2,1,0:T(8,128)(2,1)S(1)}, bf16[2,2,1664,256]{3,2,1,0:T(8,128)(2,1)S(1)}, f32[2,512,1664]{2,1,0:T(8,128)S(1)}, f32[2,512,1664]{...) custom-call(bf16[2,2,32,1664]{3,2,1,0:T(8,128)(2,1)} %get-tuple-elem, ...), custom_call_target="tpu_custom_call" | custom-call | tf_op jit(solution)/shard_map/update/pallas_call | solution.py:617
  141.5 16.3 %written.1 = (bf16[2,512,1664]{2,1,0:T(8,128)(2,1)}, bf16[2,512,1664]{2,1,0:T(8,128)(2,1)}, bf16[2,1664,512]{2,1,0:T(8,128)(2,1)}, f32[2,512,1664]{2,1,0:T(8,128...) custom-call(bf16[2,2,512,1664]{3,2,1,0:T(8,128)(2,1)S(1)} %get-tuple, ...), custom_call_target="tpu_custom_call" | custom-call | tf_op jit(solution)/shard_map/written/pallas_call | solution.py:650

commit v2 on v1

--- a/solution.py
+++ b/solution.py
@@ -42,80 +42,6 @@
     s = jax.nn.sigmoid(gate)
     silu = gate * s
     return silu, (dp * up * (s + silu * (1 - s))).astype(BF16), (dp * silu).astype(BF16)
-
-
-def forward_kernel(x_ref, dy_ref, wg, wu, wd, a0_ref, a0t_ref, h1_ref, a1t_ref, mid0t_ref, mid1t_ref, dg_ref, du_ref, wgu, wdv, mid0, sem):
-    blocks = wg.shape[2] // LANES
-    gu = [interleaved(wg, wu, l, wgu.at[l], sem.at[l]) for l in range(2)]
-    down = [pltpu.make_async_copy(wd.at[l], wdv.at[l], sem.at[2 + l]) for l in range(2)]
-    first = pl.program_id(0) == 0
-
-    @pl.when(first)
-    def _():
-        for l in range(2):
-            for c in gu[l]:
-                c.start()
-            down[l].start()
-        pltpu.make_async_copy(wgu.at[0], wgu.at[0], sem.at[0]).wait()
-
-    x = x_ref[...]
-    a0 = normed(x)
-    a0_ref[...] = a0
-    a0t_ref[...] = a0.T
-    for j in range(blocks):
-        both = dot(a0, wgu[0, :, 2 * j * LANES : 2 * (j + 1) * LANES])
-        gate, up = both[:, :LANES], both[:, LANES:]
-        mid = (gate * jax.nn.sigmoid(gate) * up).astype(BF16)
-        mid0[:, j * LANES : (j + 1) * LANES] = mid
-        mid0t_ref[j * LANES : (j + 1) * LANES, :] = mid.T
-
-    @pl.when(first)
-    def _():
-        down[0].wait()
-
-    h1 = x + dot(mid0[...], wdv[0]).astype(BF16)
-    h1_ref[...] = h1
-    a1 = normed(h1)
-    a1t_ref[...] = a1.T
-
-    @pl.when(first)
-    def _():
-        pltpu.make_async_copy(wgu.at[1], wgu.at[1], sem.at[1]).wait()
-        down[1].wait()
-
-    dy = dy_ref[...]
-    for pair, width in pairs(blocks):
-        dp2 = dot_t(dy, wdv[1, pair * LANES : (pair + width) * LANES, :]).astype(BF16).astype(F32)
-        for j in range(pair, pair + width):
-            at = slice(j * LANES, (j + 1) * LANES)
-            both = dot(a1, wgu[1, :, 2 * j * LANES : 2 * (j + 1) * LANES])
-            gate, up = both[:, :LANES], both[:, LANES:]
-            silu, dg, du = backward_of_product(gate, up, dp2[:, (j - pair) * LANES : (j - pair + 1) * LANES])
-            mid1t_ref[at, :] = (silu * up).astype(BF16).T
-            dg_ref[:, at], du_ref[:, at] = dg, du
-
-
-def forward(x, dy, wg, wu, wd, bt=256):
-    t, d = x.shape
-    ff = wg.shape[-1]
-    rows = lambda n: pl.BlockSpec((bt, n), lambda i: (i, 0))
-    cols = lambda n: pl.BlockSpec((n, bt), lambda i: (0, i))
-    shape = lambda *s: jax.ShapeDtypeStruct(s, BF16)
-    return pl.pallas_call(
-        forward_kernel,
-        grid=(t // bt,),
-        in_specs=[rows(d), rows(d), HBM, HBM, HBM],
-        out_specs=[rows(d), cols(d), rows(d), cols(d), cols(ff), cols(ff), rows(ff), rows(ff)],
-        out_shape=[shape(t, d), shape(d, t), shape(t, d), shape(d, t), shape(ff, t), shape(ff, t), shape(t, ff), shape(t, ff)],
-        scratch_shapes=[
-            pltpu.VMEM((2, d, 2 * ff), BF16),
-            pltpu.VMEM((2, ff, d), BF16),
-            pltpu.VMEM((bt, ff), BF16),
-            pltpu.SemaphoreType.DMA((4,)),
-        ],
-        compiler_params=pltpu.CompilerParams(dimension_semantics=("arbitrary",), vmem_limit_bytes=60 * 2**20),
-        name="forward",
-    )(x, dy, wg, wu, wd)
 
 
 ORDER = ((True, 0, 1), (False, 0, 1), (False, 1, 1), (True, 0, 0), (False, 0, 0), (False, 1, 0))
@@ -163,17 +89,17 @@
     return (a[...].astype(F32) + b[...].astype(F32)).astype(BF16)
 
 
-def backward_kernel(
-    a0, a0t, h1, a1t, mid0t, mid1t, dg1, du1, dy, wg, wu, wd,
-    done_g, done_d, own_g, own_d,
+def gradients_kernel(
+    x, dy, wg, wu, wd,
+    done_g, done_d, own_g, own_d, mid0t,
     gg1, gd1, gg0, gd0, r0g, r0d, r1g, r1d, r2g, r2d,
-    midt, dgu, at, av, dh, hv, wgu0, wgu1, wd0,
-    load, store, quarters, send, recv, credit,
+    midt, dgu, at, av, dh, hv, wgu0, wgu1, wdv, mid0, midt_out,
+    load, mid_store, store, quarters, send, recv, credit,
 ):
     t, d = dh.shape
-    ff = wd0.shape[0]
+    ff = wdv.shape[1]
     blocks = ff // LANES
-    bt = 256
+    bt, fb = 256, mid0.shape[0]
     half = d // 2
     p = Places(d, ff)
 
@@ -299,24 +225,81 @@
                     what(m)
 
     local = {
-        "mid1": pltpu.make_async_copy(mid1t, midt, load.at[0]),
-        "dy": pltpu.make_async_copy(dy, dh, load.at[1]),
-        "a1": pltpu.make_async_copy(a1t, at, load.at[2]),
-        "dg": pltpu.make_async_copy(dg1, dgu.at[0], load.at[3]),
-        "du": pltpu.make_async_copy(du1, dgu.at[1], load.at[4]),
-        "h1": pltpu.make_async_copy(h1, hv, load.at[5]),
-        "wg1": pltpu.make_async_copy(wg.at[1], wgu1.at[0], load.at[6]),
-        "wu1": pltpu.make_async_copy(wu.at[1], wgu1.at[1], load.at[7]),
-        "mid0": pltpu.make_async_copy(mid0t, midt, load.at[8]),
-        "wd0": pltpu.make_async_copy(wd.at[0], wd0, load.at[9]),
-        "a0": pltpu.make_async_copy(a0, av, load.at[10]),
-        "a0t": pltpu.make_async_copy(a0t, at, load.at[11]),
+        "dy": pltpu.make_async_copy(dy, dh, load.at[0]),
+        "wd0": pltpu.make_async_copy(wd.at[0], wdv.at[0], load.at[2]),
+        "wg1": pltpu.make_async_copy(wg.at[1], wgu1.at[0], load.at[3]),
+        "wu1": pltpu.make_async_copy(wu.at[1], wgu1.at[1], load.at[4]),
+        "wd1": pltpu.make_async_copy(wd.at[1], wdv.at[1], load.at[5]),
+        "mid0": pltpu.make_async_copy(mid0t, midt, load.at[6]),
     }
+    xs = [pltpu.make_async_copy(x.at[pl.ds(i, n), :], hv.at[pl.ds(i, n), :], load.at[7 + k]) for k, (i, n) in enumerate(((0, fb), (fb, t - fb)))]
+    xs[0].start()
+    for c in interleaved(wg, wu, 0, wgu0, load.at[1]):
+        c.start()
+    local["wd0"].start()
+    xs[1].start()
+    for name in ("dy", "wd1", "wg1", "wu1"):
+        local[name].start()
     p.greet()
-    for name in ("dy", "mid1", "a1", "dg", "du", "h1", "wg1", "wu1", "wd0", "a0"):
-        local[name].start()
-    for c in interleaved(wg, wu, 0, wgu0, load.at[12]):
-        c.start()
+
+    def middle_out(step):
+        return pltpu.make_async_copy(midt_out, mid0t.at[:, pl.ds(pl.multiple_of(step * fb, fb), fb)], mid_store)
+
+    def forward(step, carry):
+        rows = pl.ds(pl.multiple_of(step * fb, fb), fb)
+
+        @pl.when(step == 0)
+        def _():
+            xs[0].wait()
+            pltpu.make_async_copy(wgu0, wgu0, load.at[1]).wait()
+
+        @pl.when(step == 1)
+        def _():
+            xs[1].wait()
+
+        @pl.when(step >= 1)
+        def _():
+            middle_out(step - 1).wait()
+
+        h = hv[rows, :]
+        a = normed(h)
+        av[rows, :] = a
+        for j in range(blocks):
+            to = slice(j * LANES, (j + 1) * LANES)
+            both = dot(a, wgu0[:, 2 * j * LANES : 2 * (j + 1) * LANES])
+            gate, up = both[:, :LANES], both[:, LANES:]
+            mid = (gate * jax.nn.sigmoid(gate) * up).astype(BF16)
+            mid0[:, to] = mid
+            midt_out[to, :] = mid.T
+
+        middle_out(step).start()
+
+        @pl.when(step == 0)
+        def _():
+            local["wd0"].wait()
+
+        h = h + dot(mid0[...], wdv[0]).astype(BF16)
+        hv[rows, :] = h
+        a = normed(h)
+        at[:, rows] = a.T
+
+        @pl.when(step == 0)
+        def _():
+            for name in ("dy", "wd1", "wg1", "wu1"):
+                local[name].wait()
+
+        by_h = dh[rows, :]
+        for pair, width in pairs(blocks):
+            to = slice(pair * LANES, (pair + width) * LANES)
+            dp = dot_t(by_h, wdv[1, to, :]).astype(BF16).astype(F32)
+            gate, up = dot(a, wgu1[0, :, to]), dot(a, wgu1[1, :, to])
+            silu, dg, du = backward_of_product(gate, up, dp)
+            midt[to, rows] = (silu * up).astype(BF16).T
+            dgu[0, rows, to], dgu[1, rows, to] = dg, du
+        return carry
+
+    lax.fori_loop(0, t // fb, forward, 0)
+    middle_out(t // fb - 1).wait()
 
     def down_grad(m, gd, table):
         def body(step, carry):
@@ -351,19 +334,10 @@
 
         lax.fori_loop(0, 4, body, 0)
 
-    local["dy"].wait()
-    local["mid1"].wait()
     pl.semaphore_wait(pltpu.get_barrier_semaphore(), 3)
     down_grad(0, gd1, {2: [(c0a, 0)], 3: [(c0b, 0)]})
     local["mid0"].start()
-    local["a1"].wait()
-    local["dg"].wait()
-    local["du"].wait()
     other_grads(1, gg1, {1: [(c1, 0), (c0, 1)], 3: [(c2, 0)]})
-    local["a0t"].start()
-    local["h1"].wait()
-    local["wg1"].wait()
-    local["wu1"].wait()
 
     def states_grad(step, carry):
         rows = pl.ds(pl.multiple_of(step * bt, bt), bt)
@@ -380,15 +354,13 @@
 
     local["mid0"].wait()
     down_grad(3, gd0, {1: [(c3, 0)], 2: [(c2, 1), (c0a, 3)], 3: [(c0b, 3)]})
-    local["wd0"].wait()
-    local["a0"].wait()
-    pltpu.make_async_copy(wgu0, wgu0, load.at[12]).wait()
 
     def layer_back(step, carry):
         rows = pl.ds(pl.multiple_of(step * bt, bt), bt)
         a, by_h = av[rows, :], dh[rows, :]
+        at[:, rows] = a.T
         for pair, width in pairs(blocks):
-            dp2 = dot_t(by_h, wd0[pair * LANES : (pair + width) * LANES, :]).astype(BF16).astype(F32)
+            dp2 = dot_t(by_h, wdv[0, pair * LANES : (pair + width) * LANES, :]).astype(BF16).astype(F32)
             for j in range(pair, pair + width):
                 to = slice(j * LANES, (j + 1) * LANES)
                 both = dot(a, wgu0[:, 2 * j * LANES : 2 * (j + 1) * LANES])
@@ -398,7 +370,6 @@
         return carry
 
     lax.fori_loop(0, t // bt, layer_back, 0)
-    local["a0t"].wait()
     other_grads(4, gg0, {1: [(c4, 1), (c0, 4)], 2: [(c2, 3), (c5, 1)], 3: [(c0, 5)]})
     for what, m in [(c4, 2), (c1, 4), (c5, 2), (c1, 5), (c2, 4), (c2, 5)]:
         what(m)
@@ -406,17 +377,17 @@
         finish(m)
 
 
-def backward(a0, a0t, h1, a1t, mid0t, mid1t, dg1, du1, dy, wg, wu, wd):
+def gradients(x, dy, wg, wu, wd, bt=512):
     t, d = dy.shape
     ff = wg.shape[2]
     half = d // 2
     vmem = lambda *s: pltpu.VMEM(s, BF16)
     return pl.pallas_call(
-        backward_kernel,
-        in_specs=[HBM] * 12,
-        out_specs=[HBM] * 4,
+        gradients_kernel,
+        in_specs=[HBM] * 5,
+        out_specs=[HBM] * 5,
         out_shape=[
-            jax.ShapeDtypeStruct(s, BF16) for s in ((2, d, ff), (2, ff, half), (2, 2, half // 8, ff), (2, ff // 8, half))
+            jax.ShapeDtypeStruct(s, BF16) for s in ((2, d, ff), (2, ff, half), (2, 2, half // 8, ff), (2, ff // 8, half), (ff, t))
         ],
         scratch_shapes=[
             vmem(2, d, ff),
@@ -437,8 +408,11 @@
             vmem(t, d),
             vmem(d, 2 * ff),
             vmem(2, d, ff),
-            vmem(ff, d),
-            pltpu.SemaphoreType.DMA((13,)),
+            vmem(2, ff, d),
+            vmem(bt, ff),
+            vmem(ff, bt),
+            pltpu.SemaphoreType.DMA((9,)),
+            pltpu.SemaphoreType.DMA,
             pltpu.SemaphoreType.DMA((3,)),
             pltpu.SemaphoreType.DMA((3, 2)),
             pltpu.SemaphoreType.DMA((6, 11)),
@@ -446,8 +420,8 @@
             pltpu.SemaphoreType.REGULAR((3,)),
         ],
         compiler_params=pltpu.CompilerParams(collective_id=0, has_side_effects=True, vmem_limit_bytes=67043328),
-        name="backward",
-    )(a0, a0t, h1, a1t, mid0t, mid1t, dg1, du1, dy, wg, wu, wd)
+        name="gradients",
+    )(x, dy, wg, wu, wd)[:4]
 
 
 def update_kernel(
@@ -661,8 +635,7 @@
 def solution(mesh):
     def step(x, dy, *arrays):
         weights, m, v = (arrays[i : i + 3] for i in (0, 3, 6))
-        made = forward(x[0], dy[0], *weights)
-        summed = backward(*made, dy[0], *weights)
+        summed = gradients(x[0], dy[0], *weights)
         return tuple(written(weights, update(weights, m, v, *summed)))
 
     return jax.shard_map(

time: 158 us -> 150 us (0.949)
  Pallas kernels: 157 us -> 149 us
    pallas_call x2 -> x1, Pallas kernels: 112 us -> 104 us  [gradients(): pl.pallas_call(gradients_kernel, in_specs=[HBM] * 5, out_specs=[HBM] * 5,...]
where the time goes in v2:
time: 150 us
  Pallas kernels  149 us (99%)
    pallas_call x1, Pallas kernels, gradients(): pl.pallas_call(gradients_kernel, in_specs=[HBM] * 5, out_specs=[HBM] * 5,...  104 us
    pallas_call x1, Pallas kernels, update(): pl.pallas_call(update_kernel, in_specs=[HBM] * 13, out_specs=[VMEM] * 8,...  28.9 us
    pallas_call x1, Pallas kernels, written(): pl.pallas_call(written_kernel, in_specs=[VMEM] * 8, out_specs=[HBM] * 9,...  16.3 us

profile of v2, /device:TPU:113, one launch (start us, length us, event | category | flops | bytes accessed | tf_op | source)
XLA Modules:
  0.0 149.9 jit_solution(9613076978303457975)
XLA Ops:
  0.6 103.8 %gradients.1 = (bf16[2,512,1664]{2,1,0:T(8,128)(2,1)}, bf16[2,1664,256]{2,1,0:T(8,128)(2,1)}, bf16[2,2,32,1664]{3,2,1,0:T(8,128)(2,1)}, bf16[2,208,256]{2,1,0:T(8,128)(2,1)}, bf16[1664,2048]{1,0:T(8,128)(2,1)}) custom-call(bf16[2048,512]{1,0:T(8,128)(2,1)} %bitcast.2, bf16[2048,512]{1,0:T(8,128)(2,1)} %bitcast.3, bf16[2,512,1664]{2,1,0:T(8,128)(2,1)} %wg.3, ...), custom_call_target="tpu_custom_call" | custom-call | tf_op jit(solution)/shard_map/gradients/pallas_call | solution.py:385
  104.5 28.9 %update.1 = (bf16[2,2,512,1664]{3,2,1,0:T(8,128)(2,1)S(1)}, bf16[2,2,1664,256]{3,2,1,0:T(8,128)(2,1)S(1)}, f32[2,512,1664]{2,1,0:T(8,128)S(1)}, f32[2,512,1664]{...) custom-call(bf16[2,2,32,1664]{3,2,1,0:T(8,128)(2,1)} %get-tuple-elem, ...), custom_call_target="tpu_custom_call" | custom-call | tf_op jit(solution)/shard_map/update/pallas_call | solution.py:591
  133.4 16.3 %written.1 = (bf16[2,512,1664]{2,1,0:T(8,128)(2,1)}, bf16[2,512,1664]{2,1,0:T(8,128)(2,1)}, bf16[2,1664,512]{2,1,0:T(8,128)(2,1)}, f32[2,512,1664]{2,1,0:T(8,128...) custom-call(bf16[2,2,512,1664]{3,2,1,0:T(8,128)(2,1)S(1)} %get-tuple, ...), custom_call_target="tpu_custom_call" | custom-call | tf_op jit(solution)/shard_map/written/pallas_call | solution.py:624

commit v3 on v2

--- a/solution.py
+++ b/solution.py
@@ -45,7 +45,7 @@
 
 
 ORDER = ((True, 0, 1), (False, 0, 1), (False, 1, 1), (True, 0, 0), (False, 0, 0), (False, 1, 0))
-S0, X1, X2, Y2, Y1, Y0, YR = 0, 2, 4, 6, 8, 10, 12
+S0, X1, X2, Y2, Y1, Y0, YR = 0, 4, 6, 8, 10, 12, 14
 
 
 class Places:
@@ -116,9 +116,13 @@
             src_ref=src, dst_ref=dst, send_sem=send.at[m, kind], recv_sem=recv.at[m, kind], device_id={"dp": device}, device_id_type=MESH
         )
 
-    def s0(m, ab):
-        size = p.height(m) // 2
-        return copy(m, S0 + ab, g_ref(m, 1 - p.core, ab * size, size), part(ref_of(m, r0d, r0g), ab * size, size), p.other_core)
+    def fourth(m, ab, kept):
+        which = p.keep[ab] if kept else 1 - p.keep[ab]
+        return p.sub_at(m, ab, which), p.height(m) // 4
+
+    def s0(m, ab, kept):
+        at = fourth(m, ab, kept)
+        return copy(m, S0 + 2 * kept + ab, g_ref(m, 1 - p.core, *at), part(ref_of(m, r0d, r0g), *at), p.other_core)
 
     def x1(m, ab):
         src = part(ref_of(m, r0d, r0g), p.sub_at(m, ab, 1 - p.keep[ab]), p.height(m) // 4)
@@ -151,23 +155,33 @@
         to = own_d.at[ab] if ORDER[m][0] else own_g.at[ORDER[m][1], ab]
         return pltpu.make_async_copy(ref_of(m, r2d, r2g, ab), to, quarters.at[m - 3, ab])
 
-    def c0(m, parts=(0, 1)):
-        size = p.height(m) // 2
-        for ab in parts:
-            s0(m, ab).wait_recv()
-            r0 = part(ref_of(m, r0d, r0g), ab * size, size)
-            r0[...] = added(r0, g_ref(m, p.core, ab * size, size))
-            x1(m, ab).start()
-        for ab in parts:
-            s0(m, ab).wait_send()
-        if ORDER[m][2] and 1 in parts:
+    def pair_sum(m, ab, kept):
+        s0(m, ab, kept).wait_recv()
+        at = fourth(m, ab, kept)
+        r0 = part(ref_of(m, r0d, r0g), *at)
+        r0[...] = added(r0, g_ref(m, p.core, *at))
+
+    def c0a(m):
+        pair_sum(m, 0, 0)
+        x1(m, 0).start()
+
+    def c0b(m):
+        pair_sum(m, 1, 0)
+        x1(m, 1).start()
+
+    def c0c(m):
+        for ab in range(2):
+            pair_sum(m, ab, 1)
+        for ab in range(2):
+            for kept in range(2):
+                s0(m, ab, kept).wait_send()
+        if ORDER[m][2]:
             pl.semaphore_signal(credit.at[m], inc=1, device_id={"dp": p.other_core}, device_id_type=MESH)
 
-    def c0a(m):
-        c0(m, (0,))
-
-    def c0b(m):
-        c0(m, (1,))
+    def c0(m):
+        c0a(m)
+        c0b(m)
+        c0c(m)
 
     def c1(m):
         for ab in range(2):
@@ -276,22 +290,26 @@
 
         @pl.when(step == 0)
         def _():
-            local["wd0"].wait()
+            for name in ("wd0", "dy", "wd1"):
+                local[name].wait()
 
         h = h + dot(mid0[...], wdv[0]).astype(BF16)
+        by_h = dh[rows, :]
+        for pair, width in pairs(blocks):
+            to = slice(pair * LANES, (pair + width) * LANES)
+            dgu[1, rows, to] = dot_t(by_h, wdv[1, to, :]).astype(BF16)
         hv[rows, :] = h
         a = normed(h)
         at[:, rows] = a.T
 
         @pl.when(step == 0)
         def _():
-            for name in ("dy", "wd1", "wg1", "wu1"):
+            for name in ("wg1", "wu1"):
                 local[name].wait()
 
-        by_h = dh[rows, :]
         for pair, width in pairs(blocks):
             to = slice(pair * LANES, (pair + width) * LANES)
-            dp = dot_t(by_h, wdv[1, to, :]).astype(BF16).astype(F32)
+            dp = dgu[1, rows, to].astype(F32)
             gate, up = dot(a, wgu1[0, :, to]), dot(a, wgu1[1, :, to])
             silu, dg, du = backward_of_product(gate, up, dp)
             midt[to, rows] = (silu * up).astype(BF16).T
@@ -302,20 +320,26 @@
     middle_out(t // fb - 1).wait()
 
     def down_grad(m, gd, table):
+        sub = ff // 4
+
         def body(step, carry):
-            which = jnp.where(step < 2, 1 - p.core, p.core)
-            rows = pl.ds(pl.multiple_of((step % 2) * (ff // 2), 16), ff // 2)
+            kept, own, ab = step // 4, (step % 4) // 2, step % 2
+            which = jnp.where(own == 0, 1 - p.core, p.core)
+            keep = jnp.where(ab == 0, p.keep[0], p.keep[1])
+            at = 2 * ab + jnp.where(kept == 0, 1 - keep, keep)
+            rows = pl.ds(pl.multiple_of(at * sub, 16), sub)
             gd[which, rows, :] = dot(midt[rows, :], dh[:, pl.ds(pl.multiple_of(which * half, half), half)]).astype(BF16)
-            for ab in range(2):
-
-                @pl.when(step == ab)
-                def _():
-                    s0(m, ab).start()
+            for k in range(2):
+                for n in range(2):
+
+                    @pl.when(step == 4 * k + n)
+                    def _():
+                        s0(m, n, k).start()
 
             run(step, table)
             return carry
 
-        lax.fori_loop(0, 4, body, 0)
+        lax.fori_loop(0, 8, body, 0)
 
     def other_grads(m, gg, table):
         def body(step, carry):
@@ -326,8 +350,9 @@
 
                 @pl.when(step == 2 * n)
                 def _():
-                    for ab in range(2):
-                        s0(m + n, ab).start()
+                    for kept in range(2):
+                        for ab in range(2):
+                            s0(m + n, ab, kept).start()
 
             run(step, table)
             return carry
@@ -335,9 +360,9 @@
         lax.fori_loop(0, 4, body, 0)
 
     pl.semaphore_wait(pltpu.get_barrier_semaphore(), 3)
-    down_grad(0, gd1, {2: [(c0a, 0)], 3: [(c0b, 0)]})
+    down_grad(0, gd1, {3: [(c0a, 0)], 4: [(c0b, 0)]})
     local["mid0"].start()
-    other_grads(1, gg1, {1: [(c1, 0), (c0, 1)], 3: [(c2, 0)]})
+    other_grads(1, gg1, {0: [(c0c, 0)], 1: [(c1, 0), (c0, 1)], 3: [(c2, 0)]})
 
     def states_grad(step, carry):
         rows = pl.ds(pl.multiple_of(step * bt, bt), bt)
@@ -353,7 +378,7 @@
     lax.fori_loop(0, t // bt, states_grad, 0)
 
     local["mid0"].wait()
-    down_grad(3, gd0, {1: [(c3, 0)], 2: [(c2, 1), (c0a, 3)], 3: [(c0b, 3)]})
+    down_grad(3, gd0, {1: [(c3, 0)], 3: [(c2, 1), (c0a, 3)], 4: [(c0b, 3)]})
 
     def layer_back(step, carry):
         rows = pl.ds(pl.multiple_of(step * bt, bt), bt)
@@ -366,7 +391,7 @@
                 both = dot(a, wgu0[:, 2 * j * LANES : 2 * (j + 1) * LANES])
                 _, dg, du = backward_of_product(both[:, :LANES], both[:, LANES:], dp2[:, (j - pair) * LANES : (j - pair + 1) * LANES])
                 dgu[0, rows, to], dgu[1, rows, to] = dg, du
-        run(step, {0: [(c2, 2)], 2: [(c4, 0)], 4: [(c5, 0), (c3, 1)], 6: [(c1, 3)], 7: [(c3, 2)]})
+        run(step, {0: [(c0c, 3), (c2, 2)], 2: [(c4, 0)], 4: [(c5, 0), (c3, 1)], 6: [(c1, 3)], 7: [(c3, 2)]})
         return carry
 
     lax.fori_loop(0, t // bt, layer_back, 0)
@@ -415,8 +440,8 @@
             pltpu.SemaphoreType.DMA,
             pltpu.SemaphoreType.DMA((3,)),
             pltpu.SemaphoreType.DMA((3, 2)),
-            pltpu.SemaphoreType.DMA((6, 11)),
-            pltpu.SemaphoreType.DMA((6, 11)),
+            pltpu.SemaphoreType.DMA((6, 13)),
+            pltpu.SemaphoreType.DMA((6, 13)),
             pltpu.SemaphoreType.REGULAR((3,)),
         ],
         compiler_params=pltpu.CompilerParams(collective_id=0, has_side_effects=True, vmem_limit_bytes=67043328),

time: 150 us -> 147 us (0.980)
  Pallas kernels: 149 us -> 146 us
    pallas_call x1, Pallas kernels: 104 us -> 102 us  [gradients(): pl.pallas_call(gradients_kernel, in_specs=[HBM] * 5, out_specs=[HBM] * 5,...]
where the time goes in v3:
time: 147 us
  Pallas kernels  146 us (99%)
    pallas_call x1, Pallas kernels, gradients(): pl.pallas_call(gradients_kernel, in_specs=[HBM] * 5, out_specs=[HBM] * 5,...  102 us
    pallas_call x1, Pallas kernels, update(): pl.pallas_call(update_kernel, in_specs=[HBM] * 13, out_specs=[VMEM] * 8,...  28 us
    pallas_call x1, Pallas kernels, written(): pl.pallas_call(written_kernel, in_specs=[VMEM] * 8, out_specs=[HBM] * 9,...  16.3 us

profile of v3, /device:TPU:113, one launch (start us, length us, event | category | flops | bytes accessed | tf_op | source)
XLA Modules:
  0.0 147.0 jit_solution(1142853782550911326)
XLA Ops:
  0.6 101.8 %gradients.1 = (bf16[2,512,1664]{2,1,0:T(8,128)(2,1)}, bf16[2,1664,256]{2,1,0:T(8,128)(2,1)}, bf16[2,2,32,1664]{3,2,1,0:T(8,128)(2,1)}, bf16[2,208,256]{2,1,0:T(8,128)(2,1)}, bf16[1664,2048]{1,0:T(8,128)(2,1)}) custom-call(bf16[2048,512]{1,0:T(8,128)(2,1)} %bitcast.2, bf16[2048,512]{1,0:T(8,128)(2,1)} %bitcast.3, bf16[2,512,1664]{2,1,0:T(8,128)(2,1)} %wg.3, ...), custom_call_target="tpu_custom_call" | custom-call | tf_op jit(solution)/shard_map/gradients/pallas_call | solution.py:410
  102.4 28.0 %update.1 = (bf16[2,2,512,1664]{3,2,1,0:T(8,128)(2,1)S(1)}, bf16[2,2,1664,256]{3,2,1,0:T(8,128)(2,1)S(1)}, f32[2,512,1664]{2,1,0:T(8,128)S(1)}, f32[2,512,1664]{...) custom-call(bf16[2,2,32,1664]{3,2,1,0:T(8,128)(2,1)} %get-tuple-elem, ...), custom_call_target="tpu_custom_call" | custom-call | tf_op jit(solution)/shard_map/update/pallas_call | solution.py:616
  130.4 16.3 %written.1 = (bf16[2,512,1664]{2,1,0:T(8,128)(2,1)}, bf16[2,512,1664]{2,1,0:T(8,128)(2,1)}, bf16[2,1664,512]{2,1,0:T(8,128)(2,1)}, f32[2,512,1664]{2,1,0:T(8,128...) custom-call(bf16[2,2,512,1664]{3,2,1,0:T(8,128)(2,1)S(1)} %get-tuple, ...), custom_call_target="tpu_custom_call" | custom-call | tf_op jit(solution)/shard_map/written/pallas_call | solution.py:649

commit v4 on v3

--- a/solution.py
+++ b/solution.py
@@ -319,7 +319,7 @@
     lax.fori_loop(0, t // fb, forward, 0)
     middle_out(t // fb - 1).wait()
 
-    def down_grad(m, gd, table):
+    def down_grad(m, gd, table, steps=(0, 8)):
         sub = ff // 4
 
         def body(step, carry):
@@ -339,9 +339,9 @@
             run(step, table)
             return carry
 
-        lax.fori_loop(0, 8, body, 0)
-
-    def other_grads(m, gg, table):
+        lax.fori_loop(*steps, body, 0)
+
+    def other_grads(m, gg, table, steps=(0, 4)):
         def body(step, carry):
             which = jnp.where(step % 2 == 0, 1 - p.core, p.core)
             rows = pl.ds(pl.multiple_of(which * half, half), half)
@@ -357,12 +357,14 @@
             run(step, table)
             return carry
 
-        lax.fori_loop(0, 4, body, 0)
+        lax.fori_loop(*steps, body, 0)
 
     pl.semaphore_wait(pltpu.get_barrier_semaphore(), 3)
-    down_grad(0, gd1, {3: [(c0a, 0)], 4: [(c0b, 0)]})
+    down_grad(0, gd1, {3: [(c0a, 0), (c0b, 0)]}, (0, 4))
+    other_grads(1, gg1, {1: [(c0a, 1), (c0b, 1)]}, (0, 2))
+    down_grad(0, gd1, {}, (4, 8))
     local["mid0"].start()
-    other_grads(1, gg1, {0: [(c0c, 0)], 1: [(c1, 0), (c0, 1)], 3: [(c2, 0)]})
+    other_grads(1, gg1, {2: [(c0c, 0), (c0c, 1), (c1, 0)], 3: [(c0, 2)]}, (2, 4))
 
     def states_grad(step, carry):
         rows = pl.ds(pl.multiple_of(step * bt, bt), bt)
@@ -372,13 +374,13 @@
         scale = lax.rsqrt(jnp.mean(wide * wide, -1, keepdims=True) + 1e-6)
         along = jnp.mean(by_a * wide, -1, keepdims=True) * (scale * scale * scale)
         dh[rows, :] = dh[rows, :] + (by_a * scale - wide * along).astype(BF16)
-        run(step, {0: [(c0, 2)], 3: [(c1, 1)], 6: [(c1, 2)]})
+        run(step, {0: [(c1, 1)], 2: [(c2, 0)], 6: [(c1, 2)]})
         return carry
 
     lax.fori_loop(0, t // bt, states_grad, 0)
 
     local["mid0"].wait()
-    down_grad(3, gd0, {1: [(c3, 0)], 3: [(c2, 1), (c0a, 3)], 4: [(c0b, 3)]})
+    down_grad(3, gd0, {0: [(c2, 1)], 3: [(c3, 0), (c0a, 3)], 4: [(c0b, 3)]})
 
     def layer_back(step, carry):
         rows = pl.ds(pl.multiple_of(step * bt, bt), bt)
@@ -391,11 +393,11 @@
                 both = dot(a, wgu0[:, 2 * j * LANES : 2 * (j + 1) * LANES])
                 _, dg, du = backward_of_product(both[:, :LANES], both[:, LANES:], dp2[:, (j - pair) * LANES : (j - pair + 1) * LANES])
                 dgu[0, rows, to], dgu[1, rows, to] = dg, du
-        run(step, {0: [(c0c, 3), (c2, 2)], 2: [(c4, 0)], 4: [(c5, 0), (c3, 1)], 6: [(c1, 3)], 7: [(c3, 2)]})
+        run(step, {0: [(c0c, 3), (c2, 2)], 1: [(c3, 1)], 3: [(c4, 0)], 5: [(c5, 0)], 6: [(c1, 3)], 7: [(c3, 2)]})
         return carry
 
     lax.fori_loop(0, t // bt, layer_back, 0)
-    other_grads(4, gg0, {1: [(c4, 1), (c0, 4)], 2: [(c2, 3), (c5, 1)], 3: [(c0, 5)]})
+    other_grads(4, gg0, {1: [(c0, 4), (c4, 1)], 3: [(c0, 5), (c2, 3), (c5, 1)]})
     for what, m in [(c4, 2), (c1, 4), (c5, 2), (c1, 5), (c2, 4), (c2, 5)]:
         what(m)
     for m in range(6):

time: 147 us -> 145 us (0.986)
  Pallas kernels: 146 us -> 144 us
where the time goes in v4:
time: 145 us
  Pallas kernels  144 us (99%)
    pallas_call x1, Pallas kernels, gradients(): pl.pallas_call(gradients_kernel, in_specs=[HBM] * 5, out_specs=[HBM] * 5,...  101 us
    pallas_call x1, Pallas kernels, update(): pl.pallas_call(update_kernel, in_specs=[HBM] * 13, out_specs=[VMEM] * 8,...  26.8 us
    pallas_call x1, Pallas kernels, written(): pl.pallas_call(written_kernel, in_specs=[VMEM] * 8, out_specs=[HBM] * 9,...  16.3 us

profile of v4, /device:TPU:113, one launch (start us, length us, event | category | flops | bytes accessed | tf_op | source)
XLA Modules:
  0.0 144.7 jit_solution(6706911043503673902)
XLA Ops:
  0.6 100.7 %gradients.1 = (bf16[2,512,1664]{2,1,0:T(8,128)(2,1)}, bf16[2,1664,256]{2,1,0:T(8,128)(2,1)}, bf16[2,2,32,1664]{3,2,1,0:T(8,128)(2,1)}, bf16[2,208,256]{2,1,0:T(8,128)(2,1)}, bf16[1664,2048]{1,0:T(8,128)(2,1)}) custom-call(bf16[2048,512]{1,0:T(8,128)(2,1)} %bitcast.2, bf16[2048,512]{1,0:T(8,128)(2,1)} %bitcast.3, bf16[2,512,1664]{2,1,0:T(8,128)(2,1)} %wg.3, ...), custom_call_target="tpu_custom_call" | custom-call | tf_op jit(solution)/shard_map/gradients/pallas_call | solution.py:412
  101.4 26.8 %update.1 = (bf16[2,2,512,1664]{3,2,1,0:T(8,128)(2,1)S(1)}, bf16[2,2,1664,256]{3,2,1,0:T(8,128)(2,1)S(1)}, f32[2,512,1664]{2,1,0:T(8,128)S(1)}, f32[2,512,1664]{...) custom-call(bf16[2,2,32,1664]{3,2,1,0:T(8,128)(2,1)} %get-tuple-elem, ...), custom_call_target="tpu_custom_call" | custom-call | tf_op jit(solution)/shard_map/update/pallas_call | solution.py:618
  128.2 16.3 %written.1 = (bf16[2,512,1664]{2,1,0:T(8,128)(2,1)}, bf16[2,512,1664]{2,1,0:T(8,128)(2,1)}, bf16[2,1664,512]{2,1,0:T(8,128)(2,1)}, f32[2,512,1664]{2,1,0:T(8,128...) custom-call(bf16[2,2,512,1664]{3,2,1,0:T(8,128)(2,1)S(1)} %get-tuple, ...), custom_call_target="tpu_custom_call" | custom-call | tf_op jit(solution)/shard_map/written/pallas_call | solution.py:651

commit v5 on v4

--- a/solution.py
+++ b/solution.py
@@ -93,13 +93,13 @@
     x, dy, wg, wu, wd,
     done_g, done_d, own_g, own_d, mid0t,
     gg1, gd1, gg0, gd0, r0g, r0d, r1g, r1d, r2g, r2d,
-    midt, dgu, at, av, dh, hv, wgu0, wgu1, wdv, mid0, midt_out,
+    midt, dgu, at, av, dh, hv, wgu0, wgu1, wdv, midt_out,
     load, mid_store, store, quarters, send, recv, credit,
 ):
     t, d = dh.shape
     ff = wdv.shape[1]
     blocks = ff // LANES
-    bt, fb = 256, mid0.shape[0]
+    bt, fb = 256, midt_out.shape[1]
     half = d // 2
     p = Places(d, ff)
 
@@ -283,7 +283,7 @@
             both = dot(a, wgu0[:, 2 * j * LANES : 2 * (j + 1) * LANES])
             gate, up = both[:, :LANES], both[:, LANES:]
             mid = (gate * jax.nn.sigmoid(gate) * up).astype(BF16)
-            mid0[:, to] = mid
+            dgu[0, rows, to] = mid
             midt_out[to, :] = mid.T
 
         middle_out(step).start()
@@ -293,7 +293,7 @@
             for name in ("wd0", "dy", "wd1"):
                 local[name].wait()
 
-        h = h + dot(mid0[...], wdv[0]).astype(BF16)
+        h = h + dot(dgu[0, rows, :], wdv[0]).astype(BF16)
         by_h = dh[rows, :]
         for pair, width in pairs(blocks):
             to = slice(pair * LANES, (pair + width) * LANES)
@@ -310,7 +310,11 @@
         for pair, width in pairs(blocks):
             to = slice(pair * LANES, (pair + width) * LANES)
             dp = dgu[1, rows, to].astype(F32)
-            gate, up = dot(a, wgu1[0, :, to]), dot(a, wgu1[1, :, to])
+            if width == 1:
+                both = dot(a, jnp.concatenate([wgu1[0, :, to], wgu1[1, :, to]], 1))
+                gate, up = both[:, :LANES], both[:, LANES:]
+            else:
+                gate, up = dot(a, wgu1[0, :, to]), dot(a, wgu1[1, :, to])
             silu, dg, du = backward_of_product(gate, up, dp)
             midt[to, rows] = (silu * up).astype(BF16).T
             dgu[0, rows, to], dgu[1, rows, to] = dg, du
@@ -404,7 +408,7 @@
         finish(m)
 
 
-def gradients(x, dy, wg, wu, wd, bt=512):
+def gradients(x, dy, wg, wu, wd, bt=1024):
     t, d = dy.shape
     ff = wg.shape[2]
     half = d // 2
@@ -436,7 +440,6 @@
             vmem(d, 2 * ff),
             vmem(2, d, ff),
             vmem(2, ff, d),
-            vmem(bt, ff),
             vmem(ff, bt),
             pltpu.SemaphoreType.DMA((9,)),
             pltpu.SemaphoreType.DMA,
@@ -584,17 +587,17 @@
     for m in (3, 4, 5):
         for ab in range(2):
             mine(m, ab).start()
+    pl.semaphore_wait(pltpu.get_barrier_semaphore(), 3)
+    for m in (3, 4, 5):
+        for ab in range(2):
+            mine(m, ab).wait()
+            y2(m, ab).start()
     for m in range(6):
         own, rest = loads(m)
         if m < 3:
             own.start()
         for c in rest:
             c.start()
-    pl.semaphore_wait(pltpu.get_barrier_semaphore(), 3)
-    for m in (3, 4, 5):
-        for ab in range(2):
-            mine(m, ab).wait()
-            y2(m, ab).start()
     whole(0)
     c3(3)
     whole(1)

time: 145 us -> 144 us (level)
  no operation moved by 1% of the time
where the time goes in v5:
time: 144 us
  Pallas kernels  143 us (99%)
    pallas_call x1, Pallas kernels, gradients(): pl.pallas_call(gradients_kernel, in_specs=[HBM] * 5, out_specs=[HBM] * 5,...  99.5 us
    pallas_call x1, Pallas kernels, update(): pl.pallas_call(update_kernel, in_specs=[HBM] * 13, out_specs=[VMEM] * 8,...  26.8 us
    pallas_call x1, Pallas kernels, written(): pl.pallas_call(written_kernel, in_specs=[VMEM] * 8, out_specs=[HBM] * 9,...  16.3 us

profile of v5, /device:TPU:113, one launch (start us, length us, event | category | flops | bytes accessed | tf_op | source)
XLA Modules:
  0.0 143.5 jit_solution(16798781438303179241)
XLA Ops:
  0.6 99.5 %gradients.1 = (bf16[2,512,1664]{2,1,0:T(8,128)(2,1)}, bf16[2,1664,256]{2,1,0:T(8,128)(2,1)}, bf16[2,2,32,1664]{3,2,1,0:T(8,128)(2,1)}, bf16[2,208,256]{2,1,0:T(8,128)(2,1)}, bf16[1664,2048]{1,0:T(8,128)(2,1)}) custom-call(bf16[2048,512]{1,0:T(8,128)(2,1)} %bitcast.2, bf16[2048,512]{1,0:T(8,128)(2,1)} %bitcast.3, bf16[2,512,1664]{2,1,0:T(8,128)(2,1)} %wg.3, ...), custom_call_target="tpu_custom_call" | custom-call | tf_op jit(solution)/shard_map/gradients/pallas_call | solution.py:416
  100.2 26.8 %update.1 = (bf16[2,2,512,1664]{3,2,1,0:T(8,128)(2,1)S(1)}, bf16[2,2,1664,256]{3,2,1,0:T(8,128)(2,1)S(1)}, f32[2,512,1664]{2,1,0:T(8,128)S(1)}, f32[2,512,1664]{...) custom-call(bf16[2,2,32,1664]{3,2,1,0:T(8,128)(2,1)} %get-tuple-elem, ...), custom_call_target="tpu_custom_call" | custom-call | tf_op jit(solution)/shard_map/update/pallas_call | solution.py:621
  127.0 16.3 %written.1 = (bf16[2,512,1664]{2,1,0:T(8,128)(2,1)}, bf16[2,512,1664]{2,1,0:T(8,128)(2,1)}, bf16[2,1664,512]{2,1,0:T(8,128)(2,1)}, f32[2,512,1664]{2,1,0:T(8,128...) custom-call(bf16[2,2,512,1664]{3,2,1,0:T(8,128)(2,1)S(1)} %get-tuple, ...), custom_call_target="tpu_custom_call" | custom-call | tf_op jit(solution)/shard_map/written/pallas_call | solution.py:654
